TPU v7x, 256 devices: a whole 4x4x8 slice. The times are simulated.
256 devices in a mesh: dp: 32 (over y, x, core), mp: 8 (over z).
Axes of the slice: x: 4, y: 4, z: 8, core: 2. Of those that a mesh axis runs over, the one named last changes fastest.
Arguments:
- ref_hidden: bfloat16 [2048, 2048], P('dp', 'mp'), may hold values from -80 to 80
- proxy_hidden: bfloat16 [2048, 2048], P('dp', 'mp'), may hold values from -80 to 80
- ref_gain: float32 [2048], replicated, may hold values from 0.5 to 1.5
- proxy_gain: float32 [2048], replicated, may hold values from 0.5 to 1.5
- ref_head: bfloat16 [2048, 128256], P(None, ('dp', 'mp')), may hold values from -16 to 16
- proxy_head: bfloat16 [2048, 128256], P(None, ('dp', 'mp')), may hold values from -16 to 16
- token_ids: int32 [2048], P('dp'), may hold values from 0 to 128255
- bucket_ids: int32 [2048], P(('dp', 'mp')), may hold values from 0 to 4095
- domain_of_bucket: int32 [4096], replicated, may hold values from 0 to 21
- prior_weights: float32 [22], replicated, may hold values from 0.01 to 0.1
Outputs:
- ref_loss: float32 [2048], P(('dp', 'mp'))
- proxy_loss: float32 [2048], P(('dp', 'mp'))
- bucket_excess: float32 [4096], P(('dp', 'mp'))
- domain_log_weights: float32 [22], replicated
All inputs are finite; a program needn't handle non-finite values.
Results may differ from a plain program's by a relative error of at most 0.0035.
Values may be sent and summed in bfloat16 or wider, within the bound.
A program may use at most 64 MiB of HBM per device.

v0:
```python
import jax
import jax.numpy as jnp
from jax import lax
from jax.sharding import Mesh
from jax.sharding import PartitionSpec as P

DP_MP = ("dp_0", "dp_1", "dp_2", "mp")
DP = ("dp_0", "dp_1", "dp_2")


def in_one_piece(arrays, axis, dim, along):
    widths = [a.shape[along] for a in arrays]
    both = jnp.concatenate(arrays, axis=along)
    filled = lax.all_gather(both, axis, axis=dim, tiled=True)
    return tuple(jnp.split(filled, [sum(widths[:k]) for k in range(1, len(widths))], axis=along))


def gathered_once(x, axis):
    leaves = jax.tree.leaves(x)
    order = sorted(range(len(leaves)), key=lambda k: -leaves[k].size)
    width = (1, *leaves[order[0]].shape)[-1]
    lines = [
        jnp.pad(leaves[k].reshape(-1), (0, -leaves[k].size % width)).reshape(-1, width)
        for k in order
    ]
    both, at, found = (lax.all_gather(jnp.concatenate(lines), axis), 0, {})
    for k, line in zip(order, lines):
        piece = both[:, at : at + len(line)].reshape(len(both), -1)
        found[k] = piece[:, : leaves[k].size].reshape(-1, *leaves[k].shape)
        at += len(line)
    numbers = iter(range(len(leaves)))
    return jax.tree.map(lambda _: found[next(numbers)], x)


def merged_by_axis(x, axes, combine):
    for axis in axes:
        pieces = gathered_once(x, axis)
        x = jax.tree.map(lambda part: part[0], pieces)
        for k in range(1, lax.axis_size(axis)):
            x = combine(x, jax.tree.map(lambda part: part[k], pieces))
    return x


def over_axes(x, axes):
    for axis in axes:
        x = lax.psum(x, axis)
    return x


def normalize(hidden, gain):
    values = hidden.astype(jnp.float32)
    scale = lax.rsqrt(jnp.mean(values * values, -1, keepdims=True) + 1e-05)
    return (values * scale * gain).astype(jnp.bfloat16)


def row_stats(normed, targets, head, offset):
    logits = jnp.dot(normed, head, preferred_element_type=jnp.float32)
    top = jnp.max(logits, -1)
    total = jnp.sum(jnp.exp(logits - top[:, None]), -1)
    columns = lax.broadcasted_iota(jnp.int32, logits.shape, 1) + offset
    target = jnp.sum(jnp.where(columns == targets[:, None], logits, 0.0), -1)
    return (top, total, target)


def both_stats(norm_ref, norm_proxy, targets, ref_head, proxy_head, offset):
    first = row_stats(norm_ref, targets, ref_head, offset)
    second = row_stats(norm_proxy, targets, proxy_head, offset)
    return tuple((jnp.stack([left, right]) for left, right in zip(first, second)))


def combine_rows(earlier, later):
    top = jnp.maximum(earlier[0], later[0])
    total = earlier[1] * jnp.exp(earlier[0] - top) + later[1] * jnp.exp(later[0] - top)
    return (top, total, earlier[2] + later[2])


def on_device(
    ref_hidden,
    proxy_hidden,
    ref_gain,
    proxy_gain,
    ref_head,
    proxy_head,
    token_ids,
    bucket_ids,
    domain_of_bucket,
    prior_weights,
):
    vocab_dev = ref_head.shape[1]
    device = lax.axis_index(DP_MP)
    offset = device * vocab_dev
    own_rows = bucket_ids.shape[0]
    full_ref, full_proxy = in_one_piece((ref_hidden, proxy_hidden), "mp", 1, 0)
    norm_ref = normalize(full_ref, ref_gain)
    norm_proxy = normalize(full_proxy, proxy_gain)
    piece = (
        *in_one_piece((norm_ref, norm_proxy), DP, 0, 1),
        lax.all_gather(token_ids, DP, axis=0, tiled=True),
    )
    stats = both_stats(piece[0], piece[1], piece[2], ref_head, proxy_head, offset)
    top, total, target = tuple((fresh for fresh in stats))
    first_row = device * own_rows
    whole_top, whole_total, whole_target = merged_by_axis((top, total, target), DP_MP, combine_rows)
    own_top = lax.dynamic_slice_in_dim(whole_top, first_row, own_rows, 1)
    own_total = lax.dynamic_slice_in_dim(whole_total, first_row, own_rows, 1)
    own_target = lax.dynamic_slice_in_dim(whole_target, first_row, own_rows, 1)
    losses = own_top + jnp.log(own_total) - own_target
    excess = jnp.maximum(losses[1] - losses[0], 0.0)
    buckets = domain_of_bucket.shape[0]
    domains = prior_weights.shape[0]
    onehot = (bucket_ids[:, None] == lax.broadcasted_iota(jnp.int32, (1, buckets), 1)).astype(
        jnp.float32
    )
    table = jnp.dot(
        jnp.stack([excess, jnp.ones_like(excess)]),
        onehot,
        precision=lax.Precision.HIGHEST,
        preferred_element_type=jnp.float32,
    )
    domain_hot = (
        domain_of_bucket[:, None] == lax.broadcasted_iota(jnp.int32, (1, domains), 1)
    ).astype(jnp.float32)
    bucket_dev = buckets // lax.axis_size(DP_MP)
    first_bucket = device * bucket_dev
    full_table = over_axes(table, DP_MP)
    domain_totals = jnp.dot(
        full_table, domain_hot, precision=lax.Precision.HIGHEST, preferred_element_type=jnp.float32
    )
    own_table = lax.dynamic_slice_in_dim(full_table, first_bucket, bucket_dev, 1)
    bucket_excess = own_table[0] / jnp.maximum(own_table[1], 1.0)
    domain_excess = domain_totals[0] / jnp.maximum(domain_totals[1], 1.0)
    weights = jax.nn.softmax(jnp.log(prior_weights) + 1.0 * domain_excess)
    domain_log_weights = jnp.log(0.999 * weights + 0.001 / domains)
    return (losses[0], losses[1], bucket_excess, domain_log_weights)


def solution(mesh):
    torus = Mesh(mesh.devices.reshape(4, 4, 2, mesh.shape["mp"]), ("dp_0", "dp_1", "dp_2", "mp"))
    return jax.shard_map(
        on_device,
        mesh=torus,
        in_specs=(
            P(DP, "mp"),
            P(DP, "mp"),
            P(),
            P(),
            P(None, DP_MP),
            P(None, DP_MP),
            P(DP),
            P(DP_MP),
            P(),
            P(),
        ),
        out_specs=(P(DP_MP), P(DP_MP), P(DP_MP), P()),
        check_vma=False,
    )
```

profile of v0, /device:TPU:8, one launch (start us, length us, event | category | flops | bytes accessed | tf_op | source)
XLA Modules:
  0.0 261.2 jit_solution(11383560652746233583)
XLA Ops:
  7.2 0.9 pad_maximum_fusion.1
  8.1 29.1 %all_gather.33 = bf16[128,2048]{1,0:T(8,128)(2,1)S(1)} all-gather(bf16[128,256]{1,0:T(8,128)(2,1)S(1)} %pad_maximum_fusion.1), channel_id=1, replica_groups=mesh['dp_0'=4,'dp_1'=4,'dp_2'=2,'mp'=8] {'mp'}, dimensions={1}, use_global_device_ids=true | all-gather | bytes 589824 | tf_op jit(solution)/shard_map/all_gather | solution.py:14
  37.5 0.9 fusion.8
  38.4 0.8 pad_maximum_fusion
  39.2 1.3 dynamic-slice.1
  41.2 0.9 dynamic-update-slice
  42.0 15.8 %all-reduce.1 = s32[2048]{0:T(1024)S(1)} all-reduce(s32[2048]{0:T(1024)S(1)} %dynamic-update-slice), channel_id=1, replica_groups=mesh['dp_0'=4,'dp_1'=4,'dp_2'=2,'mp'=8] {'dp_0','dp_1','dp_2'}, use_global_device_ids=true, to_apply=%add.1 | all-reduce | flops 2048 | bytes 16384
  57.8 57.8 %all-gather.10.cloned.1.call-done = bf16[2048,4096]{1,0:T(8,128)(2,1)} async-done(((bf16[64,4096]{1,0:T(8,128)(2,1)}), bf16[2048,4096]{1,0:T(8,128)(2,1)}) %all-gather.10.cloned.1.call-update) | async-done | bytes 16777232 | tf_op jit(solution)/shard_map/all_gather | solution.py:14
  115.7 7.1 %fusion.103 = (f32[2048]{0:T(1024)S(1)}, f32[2048,501]{0,1:T(8,128)S(1)}) fusion(bf16[2048,501]{0,1:T(8,128)(2,1)S(1)} %copy-done, bf16[2048,4096]{1,0:T(8,128)(2,1)} %all-gather.10.cloned.1.call-done), kind=kOutput, calls=%fused_computation.188 | convolution fusion | flops 4203716608 | bytes 14553088 | tf_op jit(solution)/shard_map/dot_general | solution.py:57
  122.7 1.2 copy-done.2
  123.9 0.6 copy-done.3
  124.5 4.5 %fusion.104 = (f32[2048]{0:T(1024)S(1)}, f32[2048,501]{0,1:T(8,128)S(1)}) fusion(bf16[2048,501]{0,1:T(8,128)(2,1)S(1)} %copy-done.3, bf16[2048,4096]{1,0:T(8,128)(2,1)S(1)} %copy-done.2), kind=kOutput, calls=%fused_computation.189 | convolution fusion | flops 4203716608 | bytes 14565376 | tf_op jit(solution)/shard_map/dot_general | solution.py:57
  129.0 2.1 fusion.5
  131.2 12.6 %all-gather.4 = f32[4,6,2048]{2,1,0:T(8,128)S(1)} all-gather(f32[1,6,2048]{2,1,0:T(8,128)S(1)} %bitcast.321), channel_id=2, replica_groups=mesh['dp_0'=4,'dp_1'=4,'dp_2'=2,'mp'=8] {'dp_0'}, dimensions={0}, use_global_device_ids=true | all-gather | bytes 245760 | tf_op jit(solution)/shard_map/all_gather | solution.py:26
  144.0 12.3 %all-gather.5 = f32[4,6,2048]{2,1,0:T(8,128)S(1)} all-gather(f32[1,6,2048]{2,1,0:T(8,128)S(1)} %maximum_bitcast_fusion), channel_id=3, replica_groups=mesh['dp_0'=4,'dp_1'=4,'dp_2'=2,'mp'=8] {'dp_1'}, dimensions={0}, use_global_device_ids=true | all-gather | bytes 245760 | tf_op jit(solution)/shard_map/all_gather | solution.py:26
  156.4 1.9 all-gather.6
  158.4 27.0 %all-gather.7 = f32[8,6,2048]{2,1,0:T(8,128)S(1)} all-gather(f32[1,6,2048]{2,1,0:T(8,128)S(1)} %maximum_bitcast_fusion.2), channel_id=5, replica_groups=mesh['dp_0'=4,'dp_1'=4,'dp_2'=2,'mp'=8] {'mp'}, dimensions={0}, use_global_device_ids=true | all-gather | bytes 442368 | tf_op jit(solution)/shard_map/all_gather | solution.py:26
  186.6 14.4 %psum.28 = f32[2,4096]{1,0:T(2,128)S(1)} all-reduce(f32[2,4096]{1,0:T(2,128)S(1)} %fusion.14), channel_id=1, replica_groups=mesh['dp_0'=4,'dp_1'=4,'dp_2'=2,'mp'=8] {'dp_0'}, use_global_device_ids=true, to_apply=%region_8.9 | all-reduce | flops 8192 | bytes 65536 | tf_op jit(solution)/shard_map/psum | solution.py:46
  201.0 16.7 %psum.29 = f32[2,4096]{1,0:T(2,128)S(1)} all-reduce(f32[2,4096]{1,0:T(2,128)S(1)} %psum.28), channel_id=1, replica_groups=mesh['dp_0'=4,'dp_1'=4,'dp_2'=2,'mp'=8] {'dp_1'}, use_global_device_ids=true, to_apply=%region_9.10 | all-reduce | flops 8192 | bytes 65536 | tf_op jit(solution)/shard_map/psum | solution.py:46
  217.7 3.4 %psum.30 = f32[2,4096]{1,0:T(2,128)S(1)} all-reduce(f32[2,4096]{1,0:T(2,128)S(1)} %psum.29), channel_id=1, replica_groups=mesh['dp_0'=4,'dp_1'=4,'dp_2'=2,'mp'=8] {'dp_2'}, use_global_device_ids=true, to_apply=%region_10.11 | all-reduce | flops 8192 | bytes 65536 | tf_op jit(solution)/shard_map/psum | solution.py:46
  221.1 28.5 %psum.31 = f32[2,4096]{1,0:T(2,128)S(1)} all-reduce(f32[2,4096]{1,0:T(2,128)S(1)} %psum.30), channel_id=1, replica_groups=mesh['dp_0'=4,'dp_1'=4,'dp_2'=2,'mp'=8] {'mp'}, use_global_device_ids=true, to_apply=%region_11.12 | all-reduce | flops 8192 | bytes 65536 | tf_op jit(solution)/shard_map/psum | solution.py:46
  249.9 0.6 fusion.95
  250.5 1.3 fusion.92
  251.8 1.9 add_log_fusion
  (35 shorter events, 2.8 us)
Async XLA Ops:
  7.2 108.5 %copy-start = (bf16[2048,501]{0,1:T(8,128)(2,1)S(1)}, bf16[2048,501]{0,1:T(8,128)(2,1)}, u32[]{:S(2)}) copy-start(bf16[2048,501]{0,1:T(8,128)(2,1)} %param.14) | copy-start | bytes 6156292
  7.2 108.5 %all-gather.10.cloned.1.call-start = ((), (), s32[]{:S(2)}) async-start(), calls=%async_computation | async-start | bytes 17301504 | tf_op jit(solution)/shard_map/all_gather | solution.py:14
  115.6 8.2 %copy-start.2 = (bf16[2048,4096]{1,0:T(8,128)(2,1)S(1)}, bf16[2048,4096]{1,0:T(8,128)(2,1)}, u32[]{:S(2)}) copy-start(bf16[2048,4096]{1,0:T(8,128)(2,1)} %all-gather.10.cloned.1.call-done) | copy-start | bytes 50331652
  115.6 8.8 %copy-start.3 = (bf16[2048,501]{0,1:T(8,128)(2,1)S(1)}, bf16[2048,501]{0,1:T(8,128)(2,1)}, u32[]{:S(2)}) copy-start(bf16[2048,501]{0,1:T(8,128)(2,1)} %param.15) | copy-start | bytes 6156292
  129.0 57.4 %copy-start.5 = (s32[8]{0:T(128)S(1)}, s32[8]{0:T(128)}, u32[]{:S(2)}) copy-start(s32[8]{0:T(128)} %param.17) | copy-start | bytes 100
  129.0 120.6 %copy-start.4 = (s32[4096]{0:T(1024)S(1)}, s32[4096]{0:T(1024)}, u32[]{:S(2)}) copy-start(s32[4096]{0:T(1024)} %param.18) | copy-start | bytes 49156
  129.0 120.9 %copy-start.1 = (f32[22]{0:T(128)S(1)}, f32[22]{0:T(128)}, u32[]{:S(2)}) copy-start(f32[22]{0:T(128)} %param.19) | copy-start | bytes 268
Sparse Core Ops, SparseCore 0:
  39.4 76.2 all-gather.9
where the time goes:
time: 262 us; the launch traced here: 261 us
  blocking collectives  162 us (62%)
  waiting for transfers between devices  57.8 us (22%)
  between operations  14.9 us (6%)
  matrix products  12.1 us (5%)
  other arithmetic  10.6 us (4%)
  local copies, waits for them, and re-layouts  4.07 us (2%)
    psum x4, blocking collectives, over_axes(): x = lax.psum(x, axis)  62.9 us
    all_gather x1, waiting for transfers between devices, in_one_piece(): filled = lax.all_gather(both, axis, axis=dim, tiled=True)  57.8 us
    all_gather x4, blocking collectives, gathered_once(): both, at, found = (lax.all_gather(jnp.concatenate(lines), axis), 0, {})  53.8 us
    all_gather x1, blocking collectives, in_one_piece(): filled = lax.all_gather(both, axis, axis=dim, tiled=True)  29.1 us
    unnamed x1, blocking collectives  15.8 us
    dot_general x2, matrix products, row_stats(): logits = jnp.dot(normed, head, preferred_element_type=jnp.float32)  11.6 us
  transfers between devices with their start and end apart: 1, of which 1 were waited for; matrix products, arithmetic and copies ran while one was open for 1% of the time, Pallas kernels for 0%

commit v1 on v0

--- a/solution.py
+++ b/solution.py
@@ -43,7 +43,7 @@
 
 def over_axes(x, axes):
     for axis in axes:
-        x = lax.psum(x, axis)
+        x = jnp.sum(lax.all_gather(x, axis), axis=0)
     return x
 
 

time: 262 us -> 250 us (0.954)
  blocking collectives: 162 us -> 149 us
    psum x4 -> x0, blocking collectives: 62.9 us -> none  [over_axes(): x = lax.psum(x, axis)]
    all_gather x0 -> x4, blocking collectives: none -> 50.6 us  [over_axes(): x = jnp.sum(lax.all_gather(x, axis), axis=0)]
where the time goes in v1:
time: 250 us; the launch traced here: 249 us
  blocking collectives  149 us (60%)
  waiting for transfers between devices  57.8 us (23%)
  between operations  14.9 us (6%)
  matrix products  12.1 us (5%)
  other arithmetic  10.9 us (4%)
  local copies, waits for them, and re-layouts  4.07 us (2%)
    all_gather x1, waiting for transfers between devices, in_one_piece(): filled = lax.all_gather(both, axis, axis=dim, tiled=True)  57.8 us
    all_gather x4, blocking collectives, gathered_once(): both, at, found = (lax.all_gather(jnp.concatenate(lines), axis), 0, {})  53.8 us
    all_gather x4, blocking collectives, over_axes(): x = jnp.sum(lax.all_gather(x, axis), axis=0)  50.6 us
    all_gather x1, blocking collectives, in_one_piece(): filled = lax.all_gather(both, axis, axis=dim, tiled=True)  29.1 us
    unnamed x1, blocking collectives  15.8 us
    dot_general x2, matrix products, row_stats(): logits = jnp.dot(normed, head, preferred_element_type=jnp.float32)  11.6 us
  transfers between devices with their start and end apart: 1, of which 1 were waited for; matrix products, arithmetic and copies ran while one was open for 1% of the time, Pallas kernels for 0%

profile of v1, /device:TPU:8, one launch (start us, length us, event | category | flops | bytes accessed | tf_op | source)
XLA Modules:
  0.0 249.1 jit_solution(4975252972946875192)
XLA Ops:
  7.2 0.9 pad_maximum_fusion.1
  8.1 29.1 %all_gather.57 = bf16[128,2048]{1,0:T(8,128)(2,1)S(1)} all-gather(bf16[128,256]{1,0:T(8,128)(2,1)S(1)} %pad_maximum_fusion.1), channel_id=1, replica_groups=mesh['dp_0'=4,'dp_1'=4,'dp_2'=2,'mp'=8] {'mp'}, dimensions={1}, use_global_device_ids=true | all-gather | bytes 589824 | tf_op jit(solution)/shard_map/all_gather | solution.py:14
  37.5 0.9 fusion.8
  38.4 0.8 pad_maximum_fusion
  39.2 1.3 dynamic-slice.1
  41.2 0.9 dynamic-update-slice
  42.0 15.8 %all-reduce.1 = s32[2048]{0:T(1024)S(1)} all-reduce(s32[2048]{0:T(1024)S(1)} %dynamic-update-slice), channel_id=1, replica_groups=mesh['dp_0'=4,'dp_1'=4,'dp_2'=2,'mp'=8] {'dp_0','dp_1','dp_2'}, use_global_device_ids=true, to_apply=%add.1 | all-reduce | flops 2048 | bytes 16384
  57.8 57.8 %all-gather.18.cloned.1.call-done = bf16[2048,4096]{1,0:T(8,128)(2,1)} async-done(((bf16[64,4096]{1,0:T(8,128)(2,1)}), bf16[2048,4096]{1,0:T(8,128)(2,1)}) %all-gather.18.cloned.1.call-update) | async-done | bytes 16777232 | tf_op jit(solution)/shard_map/all_gather | solution.py:14
  115.7 7.1 %fusion.102 = (f32[2048]{0:T(1024)S(1)}, f32[2048,501]{0,1:T(8,128)S(1)}) fusion(bf16[2048,501]{0,1:T(8,128)(2,1)S(1)} %copy-done, bf16[2048,4096]{1,0:T(8,128)(2,1)} %all-gather.18.cloned.1.call-done), kind=kOutput, calls=%fused_computation.188 | convolution fusion | flops 4203716608 | bytes 14553088 | tf_op jit(solution)/shard_map/dot_general | solution.py:57
  122.7 1.2 copy-done.2
  123.9 0.6 copy-done.3
  124.5 4.5 %fusion.103 = (f32[2048]{0:T(1024)S(1)}, f32[2048,501]{0,1:T(8,128)S(1)}) fusion(bf16[2048,501]{0,1:T(8,128)(2,1)S(1)} %copy-done.3, bf16[2048,4096]{1,0:T(8,128)(2,1)S(1)} %copy-done.2), kind=kOutput, calls=%fused_computation.189 | convolution fusion | flops 4203716608 | bytes 14565376 | tf_op jit(solution)/shard_map/dot_general | solution.py:57
  129.0 2.1 fusion.5
  131.2 12.6 %all-gather.8 = f32[4,6,2048]{2,1,0:T(8,128)S(1)} all-gather(f32[1,6,2048]{2,1,0:T(8,128)S(1)} %bitcast.326), channel_id=2, replica_groups=mesh['dp_0'=4,'dp_1'=4,'dp_2'=2,'mp'=8] {'dp_0'}, dimensions={0}, use_global_device_ids=true | all-gather | bytes 245760 | tf_op jit(solution)/shard_map/all_gather | solution.py:26
  144.0 12.3 %all-gather.9 = f32[4,6,2048]{2,1,0:T(8,128)S(1)} all-gather(f32[1,6,2048]{2,1,0:T(8,128)S(1)} %maximum_bitcast_fusion), channel_id=3, replica_groups=mesh['dp_0'=4,'dp_1'=4,'dp_2'=2,'mp'=8] {'dp_1'}, dimensions={0}, use_global_device_ids=true | all-gather | bytes 245760 | tf_op jit(solution)/shard_map/all_gather | solution.py:26
  156.4 1.9 all-gather.10
  158.4 27.0 %all-gather.11 = f32[8,6,2048]{2,1,0:T(8,128)S(1)} all-gather(f32[1,6,2048]{2,1,0:T(8,128)S(1)} %maximum_bitcast_fusion.2), channel_id=5, replica_groups=mesh['dp_0'=4,'dp_1'=4,'dp_2'=2,'mp'=8] {'mp'}, dimensions={0}, use_global_device_ids=true | all-gather | bytes 442368 | tf_op jit(solution)/shard_map/all_gather | solution.py:26
  186.6 12.0 %all-gather.12 = f32[4,2,4096]{2,1,0:T(2,128)S(1)} all-gather(f32[1,2,4096]{2,1,0:T(2,128)S(1)} %convolution_bitcast_fusion), channel_id=6, replica_groups=mesh['dp_0'=4,'dp_1'=4,'dp_2'=2,'mp'=8] {'dp_0'}, dimensions={0}, use_global_device_ids=true | all-gather | bytes 163840 | tf_op jit(solution)/shard_map/all_gather | solution.py:46
  198.7 12.0 %all-gather.13 = f32[4,2,4096]{2,1,0:T(2,128)S(1)} all-gather(f32[1,2,4096]{2,1,0:T(2,128)S(1)} %bitcast.327), channel_id=7, replica_groups=mesh['dp_0'=4,'dp_1'=4,'dp_2'=2,'mp'=8] {'dp_1'}, dimensions={0}, use_global_device_ids=true | all-gather | bytes 163840 | tf_op jit(solution)/shard_map/all_gather | solution.py:46
  210.7 1.9 all-gather.14
  212.6 24.8 %all-gather.15 = f32[8,2,4096]{2,1,0:T(2,128)S(1)} all-gather(f32[1,2,4096]{2,1,0:T(2,128)S(1)} %bitcast.329), channel_id=9, replica_groups=mesh['dp_0'=4,'dp_1'=4,'dp_2'=2,'mp'=8] {'mp'}, dimensions={0}, use_global_device_ids=true | all-gather | bytes 294912 | tf_op jit(solution)/shard_map/all_gather | solution.py:46
  237.8 0.6 fusion.94
  238.4 1.3 fusion.91
  239.8 1.9 add_log_fusion
  (39 shorter events, 3.0 us)
Async XLA Ops:
  7.2 108.5 %copy-start = (bf16[2048,501]{0,1:T(8,128)(2,1)S(1)}, bf16[2048,501]{0,1:T(8,128)(2,1)}, u32[]{:S(2)}) copy-start(bf16[2048,501]{0,1:T(8,128)(2,1)} %param.14) | copy-start | bytes 6156292
  7.2 108.5 %all-gather.18.cloned.1.call-start = ((), (), s32[]{:S(2)}) async-start(), calls=%async_computation | async-start | bytes 17301504 | tf_op jit(solution)/shard_map/all_gather | solution.py:14
  115.6 8.2 %copy-start.2 = (bf16[2048,4096]{1,0:T(8,128)(2,1)S(1)}, bf16[2048,4096]{1,0:T(8,128)(2,1)}, u32[]{:S(2)}) copy-start(bf16[2048,4096]{1,0:T(8,128)(2,1)} %all-gather.18.cloned.1.call-done) | copy-start | bytes 50331652
  115.6 8.8 %copy-start.3 = (bf16[2048,501]{0,1:T(8,128)(2,1)S(1)}, bf16[2048,501]{0,1:T(8,128)(2,1)}, u32[]{:S(2)}) copy-start(bf16[2048,501]{0,1:T(8,128)(2,1)} %param.15) | copy-start | bytes 6156292
  129.0 57.4 %copy-start.5 = (s32[8]{0:T(128)S(1)}, s32[8]{0:T(128)}, u32[]{:S(2)}) copy-start(s32[8]{0:T(128)} %param.17) | copy-start | bytes 100
  131.1 106.4 %copy-start.4 = (s32[4096]{0:T(1024)S(1)}, s32[4096]{0:T(1024)}, u32[]{:S(2)}) copy-start(s32[4096]{0:T(1024)} %param.18) | copy-start | bytes 49156
  131.1 106.7 %copy-start.1 = (f32[22]{0:T(128)S(1)}, f32[22]{0:T(128)}, u32[]{:S(2)}) copy-start(f32[22]{0:T(128)} %param.19) | copy-start | bytes 268
Sparse Core Ops, SparseCore 0:
  39.4 76.2 all-gather.17
